TPU v7x, 32 devices: a whole 2x2x4 slice. The times are simulated.
32 devices in a mesh: ctx: 8 (over y, x, core), tp: 4 (over z).
Axes of the slice: x: 2, y: 2, z: 4, core: 2. Of those that a mesh axis runs over, the one named last changes fastest.
Arguments:
- resid: bfloat16 [16384, 4096], P('ctx', 'tp'), may hold values from -6 to 6
- sel_blocks: int32 [16], P('ctx'), may hold values from 0 to 127, as said below
- norm_gain: float32 [4096], replicated, may hold values from 0.5 to 1.5
- router_weight: float32 [4096], replicated, may hold values from -0.09375 to 0.09375
- w_query: bfloat16 [4096, 4096], P(None, 'tp'), may hold values from -0.25 to 0.25
- w_key: bfloat16 [4096, 512], P(None, 'tp'), may hold values from -4 to 4
- value_projection: bfloat16 [4096, 512], P(None, 'tp'), may hold values from -0.09375 to 0.09375
- w_out: bfloat16 [4096, 4096], P('tp'), may hold values from -0.09375 to 0.09375
Outputs:
- mixed: bfloat16 [2048, 4096], P(('ctx', 'tp'))
Inputs may be any that keep to these rules, and one draw needn't show every extreme that they name: `sel_blocks`: entries 2 * c to 2 * c + 1 are 2 different numbers from c * 16 to c * 16 + 15, increasing.
All inputs are finite; a program needn't handle non-finite values.
Results may differ from a plain program's by a relative error of at most 0.0075.
Values may be sent and summed in bfloat16 or wider, within the bound.
A program may use at most 128 MiB of HBM per device.

v0:
```python
import functools
import math

import jax
import jax.numpy as jnp
import numpy as np
from jax import lax
from jax.experimental import pallas as pl
from jax.experimental.pallas import tpu as pltpu
from jax.sharding import PartitionSpec as P

HEAD_WIDTH = 128
BLK = 128
ROPE_BASE = 500000.0
NORM_EPS = 1e-05
MASKED = -1e30
MESH = pl.DeviceIdType.MESH
ROW_CHUNKS = 4
BF16 = jnp.bfloat16
F32 = jnp.float32


def pick(sel_ref, resid_hbm, row_hbm, block_hbm, x_ref, rot, row_ref, block_ref, sem):
    picked = x_ref.shape[0] // BLK
    total_blocks = block_ref.shape[0] // 2
    before = lax.axis_index("ctx") * (resid_hbm.shape[0] // BLK)
    copies = [
        pltpu.make_async_copy(
            resid_hbm.at[pl.ds(pl.multiple_of((sel_ref[i] - before) * BLK, BLK), BLK), :],
            x_ref.at[pl.ds(i * BLK, BLK), :],
            sem.at[i],
        )
        for i in range(picked)
    ]
    tables = [
        pltpu.make_async_copy(src, dst, sem.at[picked + i])
        for i, (src, dst) in enumerate(((row_hbm, row_ref), (block_hbm, block_ref)))
    ]
    for copy in copies + tables:
        copy.start()
    for copy in tables:
        copy.wait()
    hw = HEAD_WIDTH
    flip = jnp.where(lax.broadcasted_iota(jnp.int32, (1, hw), 1) < hw // 2, -1.0, 1.0)
    for i in range(picked):
        part = slice(i * BLK, (i + 1) * BLK)
        block_cos = block_ref[pl.ds(sel_ref[i], 1), :]
        block_sin = block_ref[pl.ds(sel_ref[i] + total_blocks, 1), :]
        row_cos, row_sin = row_ref[:BLK, :], row_ref[BLK:, :]
        rot[0, part, :] = block_cos * row_cos - block_sin * row_sin
        rot[1, part, :] = (block_sin * row_cos + block_cos * row_sin) * flip
    for copy in copies:
        copy.wait()


def fused(
    tp_size, ctx_size,
    x_ref, rot, gain_hbm, router_hbm, wq_hbm, wk_hbm, wv_hbm, wo_hbm,
    out_ref,
    gain_ref, router_ref, xg, wq, wk, wv, wo, qacc, kvacc, sumsq, qs, kvs, high, total, accum, att,
    sbuf, rbuf, fin,
    w_sem, ag_send, ag_recv, kv_send, kv_recv, relay_send, pair_send, rs_send, rs_recv,
):
    me = lax.axis_index("tp")
    c = lax.axis_index("ctx")
    rows, width = xg.shape[1:]
    heads = wq.shape[1] // HEAD_WIDTH
    hw = HEAD_WIDTH
    chunk = rows // ROW_CHUNKS
    share = rows // tp_size
    pairs = ctx_size // 2
    pair = c // 2
    parity = c % 2
    has_up = me < tp_size - 1
    has_dn = me > 0

    copies = [
        pltpu.make_async_copy(src, dst, w_sem.at[i])
        for i, (src, dst) in enumerate(
            (
                (gain_hbm, gain_ref),
                (wq_hbm, wq),
                (wk_hbm, wk),
                (wv_hbm, wv),
                (router_hbm, router_ref),
                (wo_hbm, wo),
            )
        )
    ]
    for copy in copies:
        copy.start()

    barrier = pltpu.get_barrier_semaphore()

    @pl.when(has_up)
    def _():
        pl.semaphore_signal(barrier, inc=1, device_id={"tp": me + 1}, device_id_type=MESH)

    @pl.when(has_dn)
    def _():
        pl.semaphore_signal(barrier, inc=1, device_id={"tp": me - 1}, device_id_type=MESH)

    def greet(k, carry):
        peer = lax.rem(c + k, ctx_size)
        pl.semaphore_signal(barrier, inc=1, device_id={"ctx": peer}, device_id_type=MESH)
        return carry

    lax.fori_loop(1, ctx_size, greet, 0)
    pl.semaphore_wait(
        barrier, ctx_size - 1 + has_up.astype(jnp.int32) + has_dn.astype(jnp.int32)
    )

    def feature_copy(src, slot, q, direction):
        side = 0 if direction > 0 else 1
        part = pl.ds(q * chunk, chunk)
        return pltpu.make_async_remote_copy(
            src_ref=src.at[part, :],
            dst_ref=xg.at[slot, part, :],
            send_sem=ag_send.at[side, slot, q],
            recv_sem=ag_recv.at[slot, q],
            device_id={"tp": me + direction},
            device_id_type=MESH,
        )

    for q in range(ROW_CHUNKS):
        for direction, there in ((1, has_up), (-1, has_dn)):
            @pl.when(there)
            def _():
                feature_copy(x_ref, me, q, direction).start()

    xg[me] = x_ref[...]
    sumsq[...] = jnp.zeros_like(sumsq)
    qacc[...] = jnp.zeros_like(qacc)
    kvacc[...] = jnp.zeros_like(kvacc)
    for i in (0, 2, 3):
        copies[i].wait()

    def project_kv(slot, part):
        depth = pl.ds(pl.multiple_of(slot * width, width), width)
        wide = xg[slot, part, :].astype(F32)
        sumsq[part, :] += jnp.sum(wide * wide, axis=1, keepdims=True)
        scaled = (wide * gain_ref[:, depth]).astype(BF16)
        kvacc[part, :hw] += jnp.dot(scaled, wk[depth, :], preferred_element_type=F32)
        kvacc[part, hw:] += jnp.dot(scaled, wv[depth, :], preferred_element_type=F32)

    def project_q(slot):
        depth = pl.ds(pl.multiple_of(slot * width, width), width)
        scaled = (xg[slot].astype(F32) * gain_ref[:, depth]).astype(BF16)
        qacc[...] += jnp.dot(scaled, wq[depth, :], preferred_element_type=F32)

    def project_q_hop(h):
        for direction in (1, -1):
            slot = me - direction * h
            inside = jnp.logical_and(slot >= 0, slot < tp_size)

            @pl.when(jnp.logical_and(inside, jnp.logical_or(h > 0, direction > 0)))
            def _():
                project_q(slot)

    project_kv(me, slice(0, rows))
    copies[1].wait()
    halves = 2
    per_half = ROW_CHUNKS // halves

    def hop(h, carry):
        project_q_hop(h - 1)
        for q in range(ROW_CHUNKS):
            for direction, onward in ((1, has_up), (-1, has_dn)):
                slot = me - direction * h
                inside = jnp.logical_and(slot >= 0, slot < tp_size)

                @pl.when(inside)
                def _():
                    feature_copy(xg.at[slot], slot, q, direction).wait_recv()

                @pl.when(jnp.logical_and(inside, onward))
                def _():
                    feature_copy(xg.at[slot], slot, q, direction).start()

            if (q + 1) % per_half == 0:
                part = slice((q + 1 - per_half) * chunk, (q + 1) * chunk)
                for direction in (1, -1):
                    slot = me - direction * h

                    @pl.when(jnp.logical_and(slot >= 0, slot < tp_size))
                    def _():
                        project_kv(slot, part)

        return carry

    lax.fori_loop(1, tp_size, hop, 0)

    inv_rms = lax.rsqrt(sumsq[...] / (width * tp_size) + NORM_EPS)
    cosine = rot[0] * inv_rms
    sine = rot[1] * inv_rms

    def rotate(block):
        return block * cosine + pltpu.roll(block, hw // 2, 1) * sine

    kvs[c, :, :hw] = rotate(kvacc[:, :hw]).astype(BF16)
    kvs[c, :, hw:] = (kvacc[:, hw:] * inv_rms).astype(BF16)

    def kv_copy(slot, peer, send):
        return pltpu.make_async_remote_copy(
            src_ref=kvs.at[slot],
            dst_ref=kvs.at[slot],
            send_sem=send,
            recv_sem=kv_recv.at[slot],
            device_id={"ctx": peer},
            device_id_type=MESH,
        )

    def send_direct(p, carry):
        kv_copy(c, 2 * p + parity, kv_send.at[p]).start()
        return carry

    lax.fori_loop(pair + 1, pairs, send_direct, 0)

    @pl.when(parity == 0)
    def _():
        kv_copy(c, c + 1, pair_send.at[0]).start()

    project_q_hop(tp_size - 1)

    factor = math.log2(math.e) / math.sqrt(hw)
    lanes = rows
    groups = heads * share // lanes
    per_group = heads // groups
    for g in range(groups):
        turned = [
            rotate(qacc[:, h * hw:(h + 1) * hw]) * factor
            for h in range(g * per_group, (g + 1) * per_group)
        ]
        for part in range(tp_size):
            stacked = jnp.concatenate([t[part * share:(part + 1) * share] for t in turned], axis=0)
            qs[part, :, g * lanes:(g + 1) * lanes] = stacked.T.astype(BF16)

    other = c + 1 - 2 * parity

    def attend_own(part):
        key = lax.broadcasted_iota(jnp.int32, (rows, lanes), 0)
        row = lax.rem(lax.broadcasted_iota(jnp.int32, (rows, lanes), 1), share) + part * share
        allowed = key <= row
        k = kvs[c, :, :hw]
        vt = kvs[c, :, hw:].T
        for g in range(groups):
            at = slice(g * lanes, (g + 1) * lanes)
            scores = jnp.dot(k, qs[part, :, at], preferred_element_type=F32)
            scores = jnp.where(allowed, scores, MASKED)
            top = jnp.max(scores, axis=0, keepdims=True)
            expd = jnp.exp2(scores - top)
            high[:, at] = top
            total[:, at] = jnp.sum(expd, axis=0, keepdims=True)
            accum[:, at] = jnp.dot(vt, expd.astype(BF16), preferred_element_type=F32)

    def attend(part, slot):
        k = kvs[slot, :, :hw]
        vt = kvs[slot, :, hw:].T
        for g in range(groups):
            at = slice(g * lanes, (g + 1) * lanes)
            scores = jnp.dot(k, qs[part, :, at], preferred_element_type=F32)
            before = high[:, at]
            top = jnp.maximum(before, jnp.max(scores, axis=0, keepdims=True))
            shrink = jnp.exp2(before - top)
            expd = jnp.exp2(scores - top)
            high[:, at] = top
            total[:, at] = total[:, at] * shrink + jnp.sum(expd, axis=0, keepdims=True)
            accum[:, at] = accum[:, at] * shrink + jnp.dot(
                vt, expd.astype(BF16), preferred_element_type=F32
            )

    def attend_share(turn, carry):
        part = jnp.where(low, tp_size - 1 - turn, turn)
        first = turn == 0
        attend_own(part)

        def take_direct(k, carry):
            slot = 2 * (pair - 1 - k) + parity

            @pl.when(first)
            def _():
                copy = kv_copy(slot, other, relay_send.at[pair - 1 - k])
                copy.wait_recv()
                copy.start()

            attend(part, slot)
            return carry

        lax.fori_loop(0, pair, take_direct, 0)

        def take_relayed(k, carry):
            slot = 2 * (pair - k) + 1 - parity

            @pl.when(first)
            def _():
                kv_copy(slot, other, pair_send.at[0]).wait_recv()

            attend(part, slot)
            return carry

        lax.fori_loop(1 - parity, pair + 1, take_relayed, 0)

        out_rows = pl.ds(pl.multiple_of(part * share, share), share)
        for g in range(groups):
            at = slice(g * lanes, (g + 1) * lanes)
            turned = (accum[:, at] / total[:, at]).T.astype(BF16)
            for k in range(per_group):
                h = g * per_group + k
                att[out_rows, h * hw:(h + 1) * hw] = turned[k * share:(k + 1) * share]
        return carry

    low = me < tp_size // 2
    outer = jnp.logical_or(me == 0, me == tp_size - 1)

    copies[5].wait()
    columns = sbuf.shape[3]
    parts = sbuf.shape[1]

    def partial(d, n):
        return jnp.dot(
            att[pl.ds(pl.multiple_of(d * share, share), share), :],
            wo[:, pl.ds(pl.multiple_of(n * columns, columns), columns)],
            preferred_element_type=F32,
        )

    def sum_copy(d, n, direction):
        side = 0 if direction > 0 else 1
        return pltpu.make_async_remote_copy(
            src_ref=sbuf.at[d, n],
            dst_ref=rbuf.at[side, d, n],
            send_sem=rs_send.at[d, n],
            recv_sem=rs_recv.at[side, d, n],
            device_id={"tp": me + direction},
            device_id_type=MESH,
        )

    def phase(turn, carry):
        lax.fori_loop(
            jnp.where(outer, turn, jnp.minimum(turn, 1) * tp_size),
            jnp.where(outer, turn + 1, tp_size),
            attend_share,
            0,
        )

        def send_distance(k, carry):
            h = tp_size - 1 - k

            def send_part(n, carry):
                for direction, behind in ((1, has_dn), (-1, has_up)):
                    side = 0 if direction > 0 else 1
                    d = me + direction * h
                    inside = jnp.logical_and(d >= 0, d < tp_size)
                    now = jnp.where(outer, k == turn, turn == 0)

                    @pl.when(jnp.logical_and(inside, now))
                    def _():
                        fin[...] = partial(d, n)

                        @pl.when(behind)
                        def _():
                            sum_copy(d, n, direction).wait_recv()
                            fin[...] += rbuf[side, d, n].astype(F32)

                        sbuf[d, n] = fin[...].astype(BF16)
                        sum_copy(d, n, direction).start()

                return carry

            lax.fori_loop(0, parts, send_part, 0)
            return carry

        lax.fori_loop(0, tp_size - 1, send_distance, 0)
        return carry

    lax.fori_loop(0, tp_size, phase, 0)

    copies[4].wait()
    mine = pl.ds(pl.multiple_of(me * share, share), share)
    logit = jnp.zeros((share, 1), F32)
    for s in range(tp_size):
        logit += jnp.sum(
            xg[s, mine, :].astype(F32) * router_ref[:, s * width:(s + 1) * width],
            axis=1,
            keepdims=True,
        )
    gate = 1.0 / (1.0 + jnp.exp(-logit))

    for n in range(parts):
        fin[...] = partial(me, n)
        for direction, behind in ((1, has_dn), (-1, has_up)):
            side = 0 if direction > 0 else 1

            @pl.when(behind)
            def _():
                sum_copy(me, n, direction).wait_recv()
                fin[...] += rbuf[side, me, n].astype(F32)

        first = n * columns
        own = xg[first // width, mine, pl.ds(first % width, columns)].astype(F32)
        out_ref[:, first:first + columns] = (own + gate * fin[...]).astype(BF16)

    for direction, onward in ((1, has_up), (-1, has_dn)):
        for h in range(tp_size):
            slot = me - direction * h

            @pl.when(jnp.logical_and(jnp.logical_and(slot >= 0, slot < tp_size), onward))
            def _():
                for q in range(ROW_CHUNKS):
                    feature_copy(xg.at[slot], slot, q, direction).wait_send()

        for h in range(1, tp_size):
            d = me + direction * h

            @pl.when(jnp.logical_and(d >= 0, d < tp_size))
            def _():
                for n in range(parts):
                    sum_copy(d, n, direction).wait_send()

    def end_direct(p, carry):
        kv_copy(c, 2 * p + parity, kv_send.at[p]).wait_send()
        return carry

    lax.fori_loop(pair + 1, pairs, end_direct, 0)

    def end_relay(p, carry):
        kv_copy(2 * p + parity, other, relay_send.at[p]).wait_send()
        return carry

    lax.fori_loop(0, pair, end_relay, 0)

    @pl.when(parity == 0)
    def _():
        kv_copy(c, c + 1, pair_send.at[0]).wait_send()


def on_device(resid, sel_blocks, norm_gain, router_weight, w_query, w_key, value_projection, w_out):
    tp_size = lax.axis_size("tp")
    ctx_size = lax.axis_size("ctx")
    rows = sel_blocks.shape[0] * BLK
    local_rows, width = resid.shape
    total_blocks = local_rows // BLK * ctx_size
    freqs = np.exp(np.arange(HEAD_WIDTH // 2) * (-2.0 * math.log(ROPE_BASE) / HEAD_WIDTH))
    freqs = np.concatenate([freqs, freqs])[None, :]

    def table(positions):
        angles = positions[:, None] * freqs
        return jnp.asarray(np.concatenate([np.cos(angles), np.sin(angles)]).astype(np.float32))

    row_table = table(np.arange(BLK))
    block_table = table(np.arange(total_blocks) * BLK)

    smem = pl.BlockSpec(memory_space=pltpu.SMEM)
    picked, rotation = pl.pallas_call(
        pick,
        out_shape=(
            jax.ShapeDtypeStruct((rows, width), BF16),
            jax.ShapeDtypeStruct((2, rows, HEAD_WIDTH), F32),
        ),
        in_specs=[smem] + [pl.BlockSpec(memory_space=pl.ANY)] * 3,
        out_specs=(pl.BlockSpec(memory_space=pltpu.VMEM),) * 2,
        scratch_shapes=[
            pltpu.VMEM(row_table.shape, F32),
            pltpu.VMEM(block_table.shape, F32),
            pltpu.SemaphoreType.DMA((sel_blocks.shape[0] + 2,)),
        ],
        name="pick",
    )(
        sel_blocks, resid, row_table, block_table,
    )

    depth, q_width = w_query.shape
    out_width = w_out.shape[1]
    heads = q_width // HEAD_WIDTH
    share = rows // tp_size
    parts = out_width // width
    columns = width
    hw = HEAD_WIDTH
    vmem = pl.BlockSpec(memory_space=pltpu.VMEM)
    hbm = pl.BlockSpec(memory_space=pl.ANY)
    dma = pltpu.SemaphoreType.DMA
    return pl.pallas_call(
        functools.partial(fused, tp_size, ctx_size),
        out_shape=jax.ShapeDtypeStruct((share, out_width), BF16),
        in_specs=[vmem] * 2 + [hbm] * 6,
        out_specs=vmem,
        scratch_shapes=[
            pltpu.VMEM((1, depth), F32),
            pltpu.VMEM((1, depth), F32),
            pltpu.VMEM((tp_size, rows, width), BF16),
            pltpu.VMEM(w_query.shape, BF16),
            pltpu.VMEM(w_key.shape, BF16),
            pltpu.VMEM(value_projection.shape, BF16),
            pltpu.VMEM(w_out.shape, BF16),
            pltpu.VMEM((rows, q_width), F32),
            pltpu.VMEM((rows, 2 * hw), F32),
            pltpu.VMEM((rows, 1), F32),
            pltpu.VMEM((tp_size, hw, heads * share), BF16),
            pltpu.VMEM((ctx_size, rows, 2 * hw), BF16),
            pltpu.VMEM((1, heads * share), F32),
            pltpu.VMEM((1, heads * share), F32),
            pltpu.VMEM((hw, heads * share), F32),
            pltpu.VMEM((rows, q_width), BF16),
            pltpu.VMEM((tp_size, parts, share, columns), BF16),
            pltpu.VMEM((2, tp_size, parts, share, columns), BF16),
            pltpu.VMEM((share, columns), F32),
            dma((6,)),
            dma((2, tp_size, ROW_CHUNKS)),
            dma((tp_size, ROW_CHUNKS)),
            dma((ctx_size // 2,)),
            dma((ctx_size,)),
            dma((ctx_size // 2,)),
            dma((1,)),
            dma((tp_size, parts)),
            dma((2, tp_size, parts)),
        ],
        compiler_params=pltpu.CompilerParams(
            collective_id=0, has_side_effects=True, vmem_limit_bytes=60 * 1024 * 1024
        ),
        name="fused",
    )(
        picked, rotation,
        norm_gain.reshape(1, -1), router_weight.reshape(1, -1),
        w_query, w_key, value_projection, w_out,
    )


def solution(mesh):
    return jax.shard_map(
        on_device,
        mesh=mesh,
        in_specs=(
            P("ctx", "tp"),
            P("ctx"),
            P(),
            P(),
            P(None, "tp"),
            P(None, "tp"),
            P(None, "tp"),
            P("tp", None),
        ),
        out_specs=P(("ctx", "tp"), None),
        check_vma=False,
    )
```

profile of v0, /device:TPU:22, one launch (start us, length us, event | category | flops | bytes accessed | tf_op | source)
XLA Modules:
  0.0 91.4 jit_solution(8464842854988031374)
XLA Ops:
  0.0 2.7 %pick.1 = (bf16[256,1024]{1,0:T(8,128)(2,1)}, f32[2,256,128]{2,1,0:T(8,128)}) custom-call(s32[2]{0:T(128)} %sel_ref.1, bf16[2048,1024]{1,0:T(8,128)(2,1)} %resid_hbm.1, f32[256,128]{1,0:T(8,128)} %constant.4.clone.row_hbm, f32[256,128]{1,0:T(8,128)} %constant.5.clone.block_hbm), custom_call_target="tpu_custom_call" | custom-call | tf_op jit(solution)/shard_map/pick/pallas_call | solution.py:453
  2.7 86.8 %fused.1 = bf16[64,4096]{1,0:T(8,128)(2,1)} custom-call(bf16[256,1024]{1,0:T(8,128)(2,1)} %get-tuple-element.7.x_ref, f32[2,256,128]{2,1,0:T(8,128)} %get-tuple-element.8.rot, f32[1,4096]{1,0:T(1,128)} %bitcast.2, f32[1,4096]{1,0:T(1,128)} %bitcast.3, bf16[4096,1024]{1,0:T(8,128)(2,1)} %wq_hbm.1, bf16[4096,128]{1,0:T(8,128)(2,1)} %wk_hbm.1, ...), custom_call_target="tpu_custom_call" | custom-call | tf_op jit(solution)/shard_map/fused/pallas_call | solution.py:481
  89.5 1.9 %copy.12 = bf16[64,4096]{1,0:T(8,128)(2,1)} copy(bf16[64,4096]{1,0:T(8,128)(2,1)} %fused.1) | data formatting | bytes 1048576
where the time goes:
time: 92.2 us; the launch traced here: 91.4 us
  Pallas kernels  89.5 us (97%)
  local copies, waits for them, and re-layouts  1.87 us (2%)
    pallas_call x1, Pallas kernels, on_device(): pl.pallas_call(functools.partial(fused, tp_size, ctx_size), out_shape=jax...  86.8 us
    pallas_call x1, Pallas kernels, on_device(): pl.pallas_call(pick, out_shape=(jax.ShapeDtypeStruct((rows, width), BF16)...  2.72 us
    unnamed x1, local copies, waits for them, and re-layouts  1.87 us

commit v1 on v0

--- a/solution.py
+++ b/solution.py
@@ -55,11 +55,11 @@
 
 def fused(
     tp_size, ctx_size,
-    x_ref, rot, gain_hbm, router_hbm, wq_hbm, wk_hbm, wv_hbm, wo_hbm,
+    x_hbm, rot_hbm, gain_hbm, router_hbm, wq_hbm, wk_hbm, wv_hbm, wo_hbm,
     out_ref,
-    gain_ref, router_ref, xg, wq, wk, wv, wo, qacc, kvacc, sumsq, qs, kvs, high, total, accum, att,
+    rot, gain_ref, router_ref, xg, wq, wkv, wo, qacc, kvacc, sumsq, qs, kvs, high, total, accum, att,
     sbuf, rbuf, fin,
-    w_sem, ag_send, ag_recv, kv_send, kv_recv, relay_send, pair_send, rs_send, rs_recv,
+    w_sem, ag_send, ag_recv, kv_send, kv_recv, rs_send, rs_recv,
 ):
     me = lax.axis_index("tp")
     c = lax.axis_index("ctx")
@@ -68,9 +68,6 @@
     hw = HEAD_WIDTH
     chunk = rows // ROW_CHUNKS
     share = rows // tp_size
-    pairs = ctx_size // 2
-    pair = c // 2
-    parity = c % 2
     has_up = me < tp_size - 1
     has_dn = me > 0
 
@@ -78,12 +75,14 @@
         pltpu.make_async_copy(src, dst, w_sem.at[i])
         for i, (src, dst) in enumerate(
             (
+                (x_hbm, xg.at[me]),
                 (gain_hbm, gain_ref),
+                (wk_hbm, wkv.at[:, pl.ds(0, hw)]),
+                (wv_hbm, wkv.at[:, pl.ds(hw, hw)]),
                 (wq_hbm, wq),
-                (wk_hbm, wk),
-                (wv_hbm, wv),
+                (rot_hbm, rot),
+                (wo_hbm, wo),
                 (router_hbm, router_ref),
-                (wo_hbm, wo),
             )
         )
     ]
@@ -106,6 +105,7 @@
         return carry
 
     lax.fori_loop(1, ctx_size, greet, 0)
+    copies[0].wait()
     pl.semaphore_wait(
         barrier, ctx_size - 1 + has_up.astype(jnp.int32) + has_dn.astype(jnp.int32)
     )
@@ -126,13 +126,12 @@
         for direction, there in ((1, has_up), (-1, has_dn)):
             @pl.when(there)
             def _():
-                feature_copy(x_ref, me, q, direction).start()
-
-    xg[me] = x_ref[...]
+                feature_copy(xg.at[me], me, q, direction).start()
+
     sumsq[...] = jnp.zeros_like(sumsq)
     qacc[...] = jnp.zeros_like(qacc)
     kvacc[...] = jnp.zeros_like(kvacc)
-    for i in (0, 2, 3):
+    for i in (1, 2, 3):
         copies[i].wait()
 
     def project_kv(slot, part):
@@ -140,8 +139,7 @@
         wide = xg[slot, part, :].astype(F32)
         sumsq[part, :] += jnp.sum(wide * wide, axis=1, keepdims=True)
         scaled = (wide * gain_ref[:, depth]).astype(BF16)
-        kvacc[part, :hw] += jnp.dot(scaled, wk[depth, :], preferred_element_type=F32)
-        kvacc[part, hw:] += jnp.dot(scaled, wv[depth, :], preferred_element_type=F32)
+        kvacc[part, :] += jnp.dot(scaled, wkv[depth, :], preferred_element_type=F32)
 
     def project_q(slot):
         depth = pl.ds(pl.multiple_of(slot * width, width), width)
@@ -158,7 +156,7 @@
                 project_q(slot)
 
     project_kv(me, slice(0, rows))
-    copies[1].wait()
+    copies[4].wait()
     halves = 2
     per_half = ROW_CHUNKS // halves
 
@@ -188,39 +186,52 @@
 
         return carry
 
-    lax.fori_loop(1, tp_size, hop, 0)
-
-    inv_rms = lax.rsqrt(sumsq[...] / (width * tp_size) + NORM_EPS)
-    cosine = rot[0] * inv_rms
-    sine = rot[1] * inv_rms
-
-    def rotate(block):
-        return block * cosine + pltpu.roll(block, hw // 2, 1) * sine
-
-    kvs[c, :, :hw] = rotate(kvacc[:, :hw]).astype(BF16)
-    kvs[c, :, hw:] = (kvacc[:, hw:] * inv_rms).astype(BF16)
-
-    def kv_copy(slot, peer, send):
+    lax.fori_loop(1, tp_size - 1, hop, 0)
+    project_q_hop(tp_size - 2)
+    copies[5].wait()
+
+    def kv_copy(slot, q, peer, send):
+        part = pl.ds(q * chunk, chunk)
         return pltpu.make_async_remote_copy(
-            src_ref=kvs.at[slot],
-            dst_ref=kvs.at[slot],
+            src_ref=kvs.at[slot, part, :],
+            dst_ref=kvs.at[slot, part, :],
             send_sem=send,
-            recv_sem=kv_recv.at[slot],
+            recv_sem=kv_recv.at[slot, q],
             device_id={"ctx": peer},
             device_id_type=MESH,
         )
 
-    def send_direct(p, carry):
-        kv_copy(c, 2 * p + parity, kv_send.at[p]).start()
-        return carry
-
-    lax.fori_loop(pair + 1, pairs, send_direct, 0)
-
-    @pl.when(parity == 0)
-    def _():
-        kv_copy(c, c + 1, pair_send.at[0]).start()
-
-    project_q_hop(tp_size - 1)
+    last = tp_size - 1
+    for q in range(ROW_CHUNKS):
+        part = slice(q * chunk, (q + 1) * chunk)
+        for direction in (1, -1):
+            slot = me - direction * last
+
+            @pl.when(jnp.logical_and(slot >= 0, slot < tp_size))
+            def _():
+                feature_copy(xg.at[slot], slot, q, direction).wait_recv()
+                project_kv(slot, part)
+
+        inv_rms = lax.rsqrt(sumsq[part, :] / (width * tp_size) + NORM_EPS)
+        cosine = rot[0, part, :] * inv_rms
+        sine = rot[1, part, :] * inv_rms
+        rot[0, part, :] = cosine
+        rot[1, part, :] = sine
+        block = kvacc[part, :hw]
+        turned = block * cosine + pltpu.roll(block, hw // 2, 1) * sine
+        kvs[c, part, :hw] = turned.astype(BF16)
+        kvs[c, part, hw:] = (kvacc[part, hw:] * inv_rms).astype(BF16)
+
+        def send_kv(p, carry):
+            kv_copy(c, q, p, kv_send.at[p, q]).start()
+            return carry
+
+        lax.fori_loop(c + 1, ctx_size, send_kv, 0)
+
+    def rotate(block):
+        return block * rot[0] + pltpu.roll(block, hw // 2, 1) * rot[1]
+
+    project_q_hop(last)
 
     factor = math.log2(math.e) / math.sqrt(hw)
     lanes = rows
@@ -234,8 +245,6 @@
         for part in range(tp_size):
             stacked = jnp.concatenate([t[part * share:(part + 1) * share] for t in turned], axis=0)
             qs[part, :, g * lanes:(g + 1) * lanes] = stacked.T.astype(BF16)
-
-    other = c + 1 - 2 * parity
 
     def attend_own(part):
         key = lax.broadcasted_iota(jnp.int32, (rows, lanes), 0)
@@ -274,31 +283,18 @@
         first = turn == 0
         attend_own(part)
 
-        def take_direct(k, carry):
-            slot = 2 * (pair - 1 - k) + parity
+        def take(k, carry):
+            slot = c - 1 - k
 
             @pl.when(first)
             def _():
-                copy = kv_copy(slot, other, relay_send.at[pair - 1 - k])
-                copy.wait_recv()
-                copy.start()
+                for q in range(ROW_CHUNKS):
+                    kv_copy(slot, q, c, kv_send.at[c, q]).wait_recv()
 
             attend(part, slot)
             return carry
 
-        lax.fori_loop(0, pair, take_direct, 0)
-
-        def take_relayed(k, carry):
-            slot = 2 * (pair - k) + 1 - parity
-
-            @pl.when(first)
-            def _():
-                kv_copy(slot, other, pair_send.at[0]).wait_recv()
-
-            attend(part, slot)
-            return carry
-
-        lax.fori_loop(1 - parity, pair + 1, take_relayed, 0)
+        lax.fori_loop(0, c, take, 0)
 
         out_rows = pl.ds(pl.multiple_of(part * share, share), share)
         for g in range(groups):
@@ -312,7 +308,7 @@
     low = me < tp_size // 2
     outer = jnp.logical_or(me == 0, me == tp_size - 1)
 
-    copies[5].wait()
+    copies[6].wait()
     columns = sbuf.shape[3]
     parts = sbuf.shape[1]
 
@@ -374,7 +370,7 @@
 
     lax.fori_loop(0, tp_size, phase, 0)
 
-    copies[4].wait()
+    copies[7].wait()
     mine = pl.ds(pl.multiple_of(me * share, share), share)
     logit = jnp.zeros((share, 1), F32)
     for s in range(tp_size):
@@ -416,21 +412,12 @@
                 for n in range(parts):
                     sum_copy(d, n, direction).wait_send()
 
-    def end_direct(p, carry):
-        kv_copy(c, 2 * p + parity, kv_send.at[p]).wait_send()
+    def end_kv(p, carry):
+        for q in range(ROW_CHUNKS):
+            kv_copy(c, q, p, kv_send.at[p, q]).wait_send()
         return carry
 
-    lax.fori_loop(pair + 1, pairs, end_direct, 0)
-
-    def end_relay(p, carry):
-        kv_copy(2 * p + parity, other, relay_send.at[p]).wait_send()
-        return carry
-
-    lax.fori_loop(0, pair, end_relay, 0)
-
-    @pl.when(parity == 0)
-    def _():
-        kv_copy(c, c + 1, pair_send.at[0]).wait_send()
+    lax.fori_loop(c + 1, ctx_size, end_kv, 0)
 
 
 def on_device(resid, sel_blocks, norm_gain, router_weight, w_query, w_key, value_projection, w_out):
@@ -481,15 +468,15 @@
     return pl.pallas_call(
         functools.partial(fused, tp_size, ctx_size),
         out_shape=jax.ShapeDtypeStruct((share, out_width), BF16),
-        in_specs=[vmem] * 2 + [hbm] * 6,
+        in_specs=[hbm] * 8,
         out_specs=vmem,
         scratch_shapes=[
+            pltpu.VMEM((2, rows, hw), F32),
             pltpu.VMEM((1, depth), F32),
             pltpu.VMEM((1, depth), F32),
             pltpu.VMEM((tp_size, rows, width), BF16),
             pltpu.VMEM(w_query.shape, BF16),
-            pltpu.VMEM(w_key.shape, BF16),
-            pltpu.VMEM(value_projection.shape, BF16),
+            pltpu.VMEM((depth, 2 * hw), BF16),
             pltpu.VMEM(w_out.shape, BF16),
             pltpu.VMEM((rows, q_width), F32),
             pltpu.VMEM((rows, 2 * hw), F32),
@@ -503,13 +490,11 @@
             pltpu.VMEM((tp_size, parts, share, columns), BF16),
             pltpu.VMEM((2, tp_size, parts, share, columns), BF16),
             pltpu.VMEM((share, columns), F32),
-            dma((6,)),
+            dma((8,)),
             dma((2, tp_size, ROW_CHUNKS)),
             dma((tp_size, ROW_CHUNKS)),
-            dma((ctx_size // 2,)),
-            dma((ctx_size,)),
-            dma((ctx_size // 2,)),
-            dma((1,)),
+            dma((ctx_size, ROW_CHUNKS)),
+            dma((ctx_size, ROW_CHUNKS)),
             dma((tp_size, parts)),
             dma((2, tp_size, parts)),
         ],

time: 92.2 us -> 88.2 us (0.957)
  Pallas kernels: 89.5 us -> 85.3 us
    pallas_call x1, Pallas kernels: 86.8 us -> 82.6 us  [on_device(): pl.pallas_call(functools.partial(fused, tp_size, ctx_size), out_shape=jax...]
where the time goes in v1:
time: 88.2 us; the launch traced here: 87.2 us
  Pallas kernels  85.3 us (97%)
  local copies, waits for them, and re-layouts  1.87 us (2%)
    pallas_call x1, Pallas kernels, on_device(): pl.pallas_call(functools.partial(fused, tp_size, ctx_size), out_shape=jax...  82.6 us
    pallas_call x1, Pallas kernels, on_device(): pl.pallas_call(pick, out_shape=(jax.ShapeDtypeStruct((rows, width), BF16)...  2.72 us
    unnamed x1, local copies, waits for them, and re-layouts  1.87 us

profile of v1, /device:TPU:22, one launch (start us, length us, event | category | flops | bytes accessed | tf_op | source)
XLA Modules:
  0.0 87.2 jit_solution(4996645002645378185)
XLA Ops:
  0.0 2.7 %pick.1 = (bf16[256,1024]{1,0:T(8,128)(2,1)}, f32[2,256,128]{2,1,0:T(8,128)}) custom-call(s32[2]{0:T(128)} %sel_ref.1, bf16[2048,1024]{1,0:T(8,128)(2,1)} %resid_hbm.1, f32[256,128]{1,0:T(8,128)} %constant.4.clone.row_hbm, f32[256,128]{1,0:T(8,128)} %constant.5.clone.block_hbm), custom_call_target="tpu_custom_call" | custom-call | tf_op jit(solution)/shard_map/pick/pallas_call | solution.py:440
  2.7 82.6 %fused.1 = bf16[64,4096]{1,0:T(8,128)(2,1)} custom-call(bf16[256,1024]{1,0:T(8,128)(2,1)} %get-tuple-element.7.x_hbm, f32[2,256,128]{2,1,0:T(8,128)} %get-tuple-element.8.rot_hbm, f32[1,4096]{1,0:T(1,128)} %bitcast.2, f32[1,4096]{1,0:T(1,128)} %bitcast.3, bf16[4096,1024]{1,0:T(8,128)(2,1)} %wq_hbm.1, bf16[4096,128]{1,0:T(8,128)(2,1)} %wk_hbm.1, ...), custom_call_target="tpu_custom_call" | custom-call | tf_op jit(solution)/shard_map/fused/pallas_call | solution.py:468
  85.3 1.9 %copy.12 = bf16[64,4096]{1,0:T(8,128)(2,1)} copy(bf16[64,4096]{1,0:T(8,128)(2,1)} %fused.1) | data formatting | bytes 1048576

commit v2 on v1

--- a/solution.py
+++ b/solution.py
@@ -16,6 +16,7 @@
 MASKED = -1e30
 MESH = pl.DeviceIdType.MESH
 ROW_CHUNKS = 4
+SHARED_PARTS = 2
 BF16 = jnp.bfloat16
 F32 = jnp.float32
 
@@ -58,8 +59,9 @@
     x_hbm, rot_hbm, gain_hbm, router_hbm, wq_hbm, wk_hbm, wv_hbm, wo_hbm,
     out_ref,
     rot, gain_ref, router_ref, xg, wq, wkv, wo, qacc, kvacc, sumsq, qs, kvs, high, total, accum, att,
-    sbuf, rbuf, fin,
+    sbuf, rbuf, fin, wo_near, att_near,
     w_sem, ag_send, ag_recv, kv_send, kv_recv, rs_send, rs_recv,
+    ship_send, ship_recv, spread_send, pair_send, att_send, att_recv,
 ):
     me = lax.axis_index("tp")
     c = lax.axis_index("ctx")
@@ -70,6 +72,20 @@
     share = rows // tp_size
     has_up = me < tp_size - 1
     has_dn = me > 0
+    middle = jnp.logical_and(has_up, has_dn)
+    end = jnp.logical_not(middle)
+    inward = jnp.where(me == 0, 1, tp_size - 2)
+    core = c % 2
+    low_bit = c // 2 % 2
+    high_bit = c // 4 % 2
+    colour = (low_bit + high_bit) % 2
+    other = c + 1 - 2 * core
+    neighbours = (c + 2 - 4 * low_bit, c + 4 - 8 * high_bit)
+    slab = wo.shape[0] // 8
+    units = 2 * SHARED_PARTS
+    columns = sbuf.shape[3]
+    parts = sbuf.shape[1]
+    split = parts - SHARED_PARTS
 
     copies = [
         pltpu.make_async_copy(src, dst, w_sem.at[i])
@@ -110,6 +126,53 @@
         barrier, ctx_size - 1 + has_up.astype(jnp.int32) + has_dn.astype(jnp.int32)
     )
 
+    def piece_of(i, t, first=0):
+        return (
+            pl.ds(pl.multiple_of((2 * i + t % 2) * slab, slab), slab),
+            pl.ds((t // 2 + first) * columns, columns),
+        )
+
+    own_slab = 2 * colour + core
+    far_slab = 2 * (1 - colour) + core
+
+    def ship_copy(t):
+        return pltpu.make_async_remote_copy(
+            src_ref=wo_hbm.at[piece_of(own_slab, t, split)],
+            dst_ref=wo_near.at[piece_of(own_slab, t)],
+            send_sem=ship_send.at[t],
+            recv_sem=ship_recv.at[own_slab, t],
+            device_id={"tp": inward},
+            device_id_type=MESH,
+        )
+
+    def piece_copy(i, t, peer, send):
+        return pltpu.make_async_remote_copy(
+            src_ref=wo_near.at[piece_of(i, t)],
+            dst_ref=wo_near.at[piece_of(i, t)],
+            send_sem=send,
+            recv_sem=ship_recv.at[i, t],
+            device_id={"ctx": peer},
+            device_id_type=MESH,
+        )
+
+    def spread_copy(t):
+        return piece_copy(own_slab, t, neighbours[t // 2 % 2], spread_send.at[t])
+
+    def spread(t):
+        spread_copy(t).wait_recv()
+        spread_copy(t).start()
+        piece_copy(own_slab, t, other, pair_send.at[0, t]).start()
+
+    def pass_on(t):
+        copy = piece_copy(far_slab, t, other, pair_send.at[1, t])
+        copy.wait_recv()
+        copy.start()
+
+    def have(n):
+        for i in (2 * colour + 1 - core, 2 * (1 - colour) + 1 - core):
+            for t in (2 * n, 2 * n + 1):
+                piece_copy(i, t, other, pair_send.at[0, t]).wait_recv()
+
     def feature_copy(src, slot, q, direction):
         side = 0 if direction > 0 else 1
         part = pl.ds(q * chunk, chunk)
@@ -128,6 +191,11 @@
             def _():
                 feature_copy(xg.at[me], me, q, direction).start()
 
+    @pl.when(end)
+    def _():
+        for t in range(units):
+            ship_copy(t).start()
+
     sumsq[...] = jnp.zeros_like(sumsq)
     qacc[...] = jnp.zeros_like(qacc)
     kvacc[...] = jnp.zeros_like(kvacc)
@@ -162,6 +230,11 @@
 
     def hop(h, carry):
         project_q_hop(h - 1)
+
+        @pl.when(jnp.logical_and(middle, h == tp_size - 2))
+        def _():
+            spread(0)
+
         for q in range(ROW_CHUNKS):
             for direction, onward in ((1, has_up), (-1, has_dn)):
                 slot = me - direction * h
@@ -189,6 +262,7 @@
     lax.fori_loop(1, tp_size - 1, hop, 0)
     project_q_hop(tp_size - 2)
     copies[5].wait()
+
 
     def kv_copy(slot, q, peer, send):
         part = pl.ds(q * chunk, chunk)
@@ -230,6 +304,10 @@
 
     def rotate(block):
         return block * rot[0] + pltpu.roll(block, hw // 2, 1) * rot[1]
+
+    @pl.when(middle)
+    def _():
+        spread(1)
 
     project_q_hop(last)
 
@@ -246,55 +324,93 @@
             stacked = jnp.concatenate([t[part * share:(part + 1) * share] for t in turned], axis=0)
             qs[part, :, g * lanes:(g + 1) * lanes] = stacked.T.astype(BF16)
 
-    def attend_own(part):
-        key = lax.broadcasted_iota(jnp.int32, (rows, lanes), 0)
-        row = lax.rem(lax.broadcasted_iota(jnp.int32, (rows, lanes), 1), share) + part * share
-        allowed = key <= row
-        k = kvs[c, :, :hw]
-        vt = kvs[c, :, hw:].T
+    def attend(part, slot, count, opening):
+        block = kvs[pl.ds(slot, count)].reshape(count * rows, 2 * hw)
+        keys = block[:, :hw]
+        vt = block[:, hw:].T
+        if opening:
+            key = lax.broadcasted_iota(jnp.int32, (rows, lanes), 0)
+            row = lax.rem(lax.broadcasted_iota(jnp.int32, (rows, lanes), 1), share)
+            allowed = key <= row + part * share
         for g in range(groups):
             at = slice(g * lanes, (g + 1) * lanes)
-            scores = jnp.dot(k, qs[part, :, at], preferred_element_type=F32)
-            scores = jnp.where(allowed, scores, MASKED)
+            scores = jnp.dot(keys, qs[part, :, at], preferred_element_type=F32)
+            if opening:
+                own = jnp.where(allowed, scores[(count - 1) * rows:], MASKED)
+                if count > 1:
+                    own = jnp.concatenate([scores[:(count - 1) * rows], own], axis=0)
+                scores = own
             top = jnp.max(scores, axis=0, keepdims=True)
+            if not opening:
+                before = high[:, at]
+                top = jnp.maximum(before, top)
             expd = jnp.exp2(scores - top)
+            summed = jnp.sum(expd, axis=0, keepdims=True)
+            mixed = jnp.dot(vt, expd.astype(BF16), preferred_element_type=F32)
+            if not opening:
+                shrink = jnp.exp2(before - top)
+                summed = total[:, at] * shrink + summed
+                mixed = accum[:, at] * shrink + mixed
             high[:, at] = top
-            total[:, at] = jnp.sum(expd, axis=0, keepdims=True)
-            accum[:, at] = jnp.dot(vt, expd.astype(BF16), preferred_element_type=F32)
-
-    def attend(part, slot):
-        k = kvs[slot, :, :hw]
-        vt = kvs[slot, :, hw:].T
-        for g in range(groups):
-            at = slice(g * lanes, (g + 1) * lanes)
-            scores = jnp.dot(k, qs[part, :, at], preferred_element_type=F32)
-            before = high[:, at]
-            top = jnp.maximum(before, jnp.max(scores, axis=0, keepdims=True))
-            shrink = jnp.exp2(before - top)
-            expd = jnp.exp2(scores - top)
-            high[:, at] = top
-            total[:, at] = total[:, at] * shrink + jnp.sum(expd, axis=0, keepdims=True)
-            accum[:, at] = accum[:, at] * shrink + jnp.dot(
-                vt, expd.astype(BF16), preferred_element_type=F32
-            )
+            total[:, at] = summed
+            accum[:, at] = mixed
+
+    sizes = [size for size in (8, 4, 2, 1) if size <= ctx_size]
+    opening = jnp.int32(1)
+    for size in reversed(sizes):
+        opening = jnp.where(c + 1 >= size, size, opening)
+    rest = c + 1 - opening
+
+    def attend_all(part):
+        for size in sizes:
+            @pl.when(opening == size)
+            def _():
+                attend(part, c + 1 - size, size, True)
+
+        left = rest
+        if ctx_size > sizes[0]:
+            def one(k, carry):
+                attend(part, rest - (k + 1) * sizes[0], sizes[0], False)
+                return carry
+
+            lax.fori_loop(0, rest // sizes[0], one, 0)
+            left = lax.rem(rest, sizes[0])
+        for size in sizes[1:]:
+            if 2 * size < ctx_size:
+                @pl.when(left >= size)
+                def _():
+                    attend(part, left - size, size, False)
+
+                left = lax.rem(left, size)
 
     def attend_share(turn, carry):
         part = jnp.where(low, tp_size - 1 - turn, turn)
         first = turn == 0
-        attend_own(part)
-
-        def take(k, carry):
-            slot = c - 1 - k
-
-            @pl.when(first)
-            def _():
+
+        @pl.when(jnp.logical_and(middle, first))
+        def _():
+            spread(2)
+
+        @pl.when(first)
+        def _():
+            def take(slot, carry):
                 for q in range(ROW_CHUNKS):
                     kv_copy(slot, q, c, kv_send.at[c, q]).wait_recv()
-
-            attend(part, slot)
-            return carry
-
-        lax.fori_loop(0, c, take, 0)
+                return carry
+
+            lax.fori_loop(0, c, take, 0)
+
+        attend_all(part)
+
+        @pl.when(jnp.logical_and(middle, turn == 0))
+        def _():
+            spread(3)
+            pass_on(0)
+            pass_on(1)
+
+        @pl.when(jnp.logical_and(middle, turn == tp_size - 2))
+        def _():
+            pass_on(2)
 
         out_rows = pl.ds(pl.multiple_of(part * share, share), share)
         for g in range(groups):
@@ -309,8 +425,6 @@
     outer = jnp.logical_or(me == 0, me == tp_size - 1)
 
     copies[6].wait()
-    columns = sbuf.shape[3]
-    parts = sbuf.shape[1]
 
     def partial(d, n):
         return jnp.dot(
@@ -330,6 +444,37 @@
             device_id_type=MESH,
         )
 
+    def att_copy(d, direction):
+        return pltpu.make_async_remote_copy(
+            src_ref=att.at[pl.ds(pl.multiple_of(d * share, share), share), :],
+            dst_ref=att_near.at[d],
+            send_sem=att_send.at[d],
+            recv_sem=att_recv.at[d],
+            device_id={"tp": me + direction},
+            device_id_type=MESH,
+        )
+
+    def at_end(k):
+        return jnp.logical_or(k == 0, k == tp_size - 1)
+
+    def add_behind(d, n, direction, behind, shared, first):
+        side = 0 if direction > 0 else 1
+        near = jnp.logical_and(behind, jnp.logical_and(shared, at_end(me - direction)))
+
+        @pl.when(near)
+        def _():
+            @pl.when(first)
+            def _():
+                att_copy(d, direction).wait_recv()
+
+            cols = pl.ds(pl.multiple_of((n - split) * columns, columns), columns)
+            fin[...] += jnp.dot(att_near[d], wo_near[:, cols], preferred_element_type=F32)
+
+        @pl.when(jnp.logical_and(behind, jnp.logical_not(near)))
+        def _():
+            sum_copy(d, n, direction).wait_recv()
+            fin[...] += rbuf[side, d, n].astype(F32)
+
     def phase(turn, carry):
         lax.fori_loop(
             jnp.where(outer, turn, jnp.minimum(turn, 1) * tp_size),
@@ -338,25 +483,36 @@
             0,
         )
 
+
         def send_distance(k, carry):
             h = tp_size - 1 - k
 
             def send_part(n, carry):
+                opening_part = jnp.logical_and(middle, jnp.logical_and(turn == 0, k == 1))
+
+                @pl.when(jnp.logical_and(opening_part, n == 1))
+                def _():
+                    pass_on(units - 1)
+
+                for i in range(SHARED_PARTS):
+                    @pl.when(jnp.logical_and(opening_part, n == split + i))
+                    def _():
+                        have(i)
+
                 for direction, behind in ((1, has_dn), (-1, has_up)):
-                    side = 0 if direction > 0 else 1
                     d = me + direction * h
                     inside = jnp.logical_and(d >= 0, d < tp_size)
-                    now = jnp.where(outer, k == turn, turn == 0)
-
-                    @pl.when(jnp.logical_and(inside, now))
+                    now = jnp.logical_and(inside, jnp.where(outer, k == turn, turn == 0))
+                    shared = n >= split
+
+                    @pl.when(jnp.logical_and(now, jnp.logical_and(end, n == split)))
+                    def _():
+                        att_copy(d, direction).start()
+
+                    @pl.when(jnp.logical_and(now, jnp.logical_or(middle, n < split)))
                     def _():
                         fin[...] = partial(d, n)
-
-                        @pl.when(behind)
-                        def _():
-                            sum_copy(d, n, direction).wait_recv()
-                            fin[...] += rbuf[side, d, n].astype(F32)
-
+                        add_behind(d, n, direction, behind, shared, n == split)
                         sbuf[d, n] = fin[...].astype(BF16)
                         sum_copy(d, n, direction).start()
 
@@ -384,12 +540,7 @@
     for n in range(parts):
         fin[...] = partial(me, n)
         for direction, behind in ((1, has_dn), (-1, has_up)):
-            side = 0 if direction > 0 else 1
-
-            @pl.when(behind)
-            def _():
-                sum_copy(me, n, direction).wait_recv()
-                fin[...] += rbuf[side, me, n].astype(F32)
+            add_behind(me, n, direction, behind, n >= split, n == split)
 
         first = n * columns
         own = xg[first // width, mine, pl.ds(first % width, columns)].astype(F32)
@@ -409,8 +560,17 @@
 
             @pl.when(jnp.logical_and(d >= 0, d < tp_size))
             def _():
-                for n in range(parts):
+                for n in range(split):
                     sum_copy(d, n, direction).wait_send()
+
+                @pl.when(middle)
+                def _():
+                    for n in range(split, parts):
+                        sum_copy(d, n, direction).wait_send()
+
+                @pl.when(end)
+                def _():
+                    att_copy(d, direction).wait_send()
 
     def end_kv(p, carry):
         for q in range(ROW_CHUNKS):
@@ -418,6 +578,18 @@
         return carry
 
     lax.fori_loop(c + 1, ctx_size, end_kv, 0)
+
+    @pl.when(end)
+    def _():
+        for t in range(units):
+            ship_copy(t).wait_send()
+
+    @pl.when(middle)
+    def _():
+        for t in range(units):
+            spread_copy(t).wait_send()
+            piece_copy(own_slab, t, other, pair_send.at[0, t]).wait_send()
+            piece_copy(far_slab, t, other, pair_send.at[1, t]).wait_send()
 
 
 def on_device(resid, sel_blocks, norm_gain, router_weight, w_query, w_key, value_projection, w_out):
@@ -490,6 +662,8 @@
             pltpu.VMEM((tp_size, parts, share, columns), BF16),
             pltpu.VMEM((2, tp_size, parts, share, columns), BF16),
             pltpu.VMEM((share, columns), F32),
+            pltpu.VMEM((w_out.shape[0], SHARED_PARTS * columns), BF16),
+            pltpu.VMEM((tp_size, share, q_width), BF16),
             dma((8,)),
             dma((2, tp_size, ROW_CHUNKS)),
             dma((tp_size, ROW_CHUNKS)),
@@ -497,6 +671,12 @@
             dma((ctx_size, ROW_CHUNKS)),
             dma((tp_size, parts)),
             dma((2, tp_size, parts)),
+            dma((2 * SHARED_PARTS,)),
+            dma((4, 2 * SHARED_PARTS)),
+            dma((2 * SHARED_PARTS,)),
+            dma((2, 2 * SHARED_PARTS)),
+            dma((tp_size,)),
+            dma((tp_size,)),
         ],
         compiler_params=pltpu.CompilerParams(
             collective_id=0, has_side_effects=True, vmem_limit_bytes=60 * 1024 * 1024

time: 88.2 us -> 85.3 us (0.967)
  Pallas kernels: 85.3 us -> 83.2 us
    pallas_call x1, Pallas kernels: 82.6 us -> 80.5 us  [on_device(): pl.pallas_call(functools.partial(fused, tp_size, ctx_size), out_shape=jax...]
where the time goes in v2:
time: 85.3 us; the launch traced here: 85.1 us
  Pallas kernels  83.2 us (98%)
  local copies, waits for them, and re-layouts  1.87 us (2%)
    pallas_call x1, Pallas kernels, on_device(): pl.pallas_call(functools.partial(fused, tp_size, ctx_size), out_shape=jax...  80.5 us
    pallas_call x1, Pallas kernels, on_device(): pl.pallas_call(pick, out_shape=(jax.ShapeDtypeStruct((rows, width), BF16)...  2.72 us
    unnamed x1, local copies, waits for them, and re-layouts  1.87 us

profile of v2, /device:TPU:22, one launch (start us, length us, event | category | flops | bytes accessed | tf_op | source)
XLA Modules:
  0.0 85.1 jit_solution(12733538329058998307)
XLA Ops:
  0.0 2.7 %pick.1 = (bf16[256,1024]{1,0:T(8,128)(2,1)}, f32[2,256,128]{2,1,0:T(8,128)}) custom-call(s32[2]{0:T(128)} %sel_ref.1, bf16[2048,1024]{1,0:T(8,128)(2,1)} %resid_hbm.1, f32[256,128]{1,0:T(8,128)} %constant.4.clone.row_hbm, f32[256,128]{1,0:T(8,128)} %constant.5.clone.block_hbm), custom_call_target="tpu_custom_call" | custom-call | tf_op jit(solution)/shard_map/pick/pallas_call | solution.py:612
  2.7 80.5 %fused.1 = bf16[64,4096]{1,0:T(8,128)(2,1)} custom-call(bf16[256,1024]{1,0:T(8,128)(2,1)} %get-tuple-element.7.x_hbm, f32[2,256,128]{2,1,0:T(8,128)} %get-tuple-element.8.rot_hbm, f32[1,4096]{1,0:T(1,128)} %bitcast.2, f32[1,4096]{1,0:T(1,128)} %bitcast.3, bf16[4096,1024]{1,0:T(8,128)(2,1)} %wq_hbm.1, bf16[4096,128]{1,0:T(8,128)(2,1)} %wk_hbm.1, ...), custom_call_target="tpu_custom_call" | custom-call | tf_op jit(solution)/shard_map/fused/pallas_call | solution.py:640
  83.2 1.9 %copy.12 = bf16[64,4096]{1,0:T(8,128)(2,1)} copy(bf16[64,4096]{1,0:T(8,128)(2,1)} %fused.1) | data formatting | bytes 1048576
